TPU v7x, 32 devices: a whole 2x2x4 slice. The times are simulated.
32 devices in a mesh: mesh: 8 (over z, y), pts: 4 (over x, core).
Axes of the slice: x: 2, y: 2, z: 4, core: 2. Of those that a mesh axis runs over, the one named last changes fastest.
Arguments:
- inputs: float32 [32768, 8], P(('mesh', 'pts')), may hold values from -6 to 6
- target: float32 [32768, 4], P(('mesh', 'pts')), may hold values from -6 to 6
- lengths: int32 [8, 4], P('mesh'), may hold values from 1 to 2048, 4096 in all within a row
- step_count: int32 [1], replicated, may hold values from 2 to 20
- muon_weight: float32 [2, 5, 256, 256], P(None, None, ('mesh', 'pts')), may hold values from -0.375 to 0.375
- muon_moment: float32 [2, 5, 256, 256], P(None, None, ('mesh', 'pts')), may hold values from -0.0017089844 to 0.0017089844
- adam_weight: float32 [18848], P(('mesh', 'pts'))
- adam_first: float32 [18848], P(('mesh', 'pts')), may hold values from -0.0004272461 to 0.0004272461
- adam_second: float32 [18848], P(('mesh', 'pts')), may hold values from 2e-11 to 4e-09
Outputs:
- new_muon_weight: float32 [2, 5, 256, 256], P(None, None, ('mesh', 'pts'))
- new_muon_moment: float32 [2, 5, 256, 256], P(None, None, ('mesh', 'pts'))
- new_adam_weight: float32 [18848], P(('mesh', 'pts'))
- new_adam_first: float32 [18848], P(('mesh', 'pts'))
- new_adam_second: float32 [18848], P(('mesh', 'pts'))
- step_loss: float32 [], replicated
- clip_norm: float32 [], replicated
Inputs may be any that keep to these rules, and one draw needn't show every extreme that they name: Each group's 4 lengths sum to 4096, and the largest of each group is exactly half of that.
All inputs are finite; a program needn't handle non-finite values.
Results may differ from a plain program's by a relative error of at most 0.0003.
Values sent between devices are 32-bit elements; how exact they have to be, the bound alone decides.
A program may use at most 192 MiB of HBM per device.

v0:
```python
from functools import partial
import math
import jax
import jax.numpy as jnp
from jax import lax
from jax.sharding import PartitionSpec as P

C = 256
H = 8
DH = 32
S = 64
IN = 8
OUT = 4
L = 2
HIGH = lax.Precision.HIGHEST
ns_a = 3.4445
ns_b = -4.775
ns_c = 2.0315
peak_rate = 0.3
warm_steps = 12.0
total_steps = 40.0


def layout():
    pieces = [
        ("emb_w", (IN, C)),
        ("emb_b", (C,)),
        ("head_w", (C, OUT)),
        ("head_b", (OUT,)),
        ("fin", (2, C)),
        ("qkv", (L, 3, DH, DH)),
        ("slice_w", (L, DH, S)),
        ("slice_b", (L, S)),
        ("temp", (L, H)),
        ("vec", (L, 9, C)),
    ]
    places = {}
    offset = 0
    for label_text, extent in pieces:
        places[label_text] = (offset, extent)
        offset = offset + math.prod(extent)
    return places


def unpack(packed):
    return {
        label_text: packed[offset : offset + math.prod(extent)].reshape(extent)
        for label_text, (offset, extent) in layout().items()
    }


def matmul(left, right):
    return jnp.dot(left, right, precision=HIGH)


def norm_rows(values, gain, shift):
    centre = values - jnp.mean(values, axis=-1, keepdims=True)
    spread = jnp.mean(centre * centre, axis=-1, keepdims=True)
    return centre * lax.rsqrt(spread + 1e-05) * gain + shift


def mesh_mask(lengths_row, first, points):
    ends = jnp.cumsum(lengths_row)
    starts = ends - lengths_row
    position = first + jnp.arange(points, dtype=jnp.int32)
    inside = (position[:, None] >= starts[None, :]) & (position[:, None] < ends[None, :])
    return inside.astype(jnp.float32)


def embed_piece(inputs, packed):
    params = unpack(packed)
    return matmul(inputs, params["emb_w"]) + params["emb_b"]


def slice_piece(hidden, matrices, packed, layer_index, onehot):
    params = unpack(packed)
    vectors = params["vec"][layer_index]
    points = hidden.shape[0]
    normed = norm_rows(hidden, vectors[0], vectors[1])
    features = (matmul(normed, matrices[0]) + vectors[2]).reshape(points, H, DH)
    routed = (matmul(normed, matrices[1]) + vectors[3]).reshape(points, H, DH)
    logits = jnp.einsum("phd,ds->phs", routed, params["slice_w"][layer_index], precision=HIGH)
    logits = (logits + params["slice_b"][layer_index]) / params["temp"][layer_index][:, None]
    weights = jax.nn.softmax(logits, axis=-1)
    numerator = jnp.einsum("pm,phs,phd->mhsd", onehot, weights, features, precision=HIGH)
    denominator = jnp.einsum("pm,phs->mhs", onehot, weights, precision=HIGH)
    return (weights, numerator, denominator)


def mix_piece(numerator, denominator, packed, layer_index):
    triple = unpack(packed)["qkv"][layer_index]
    tokens = numerator / (denominator[..., None] + 1e-05)
    queries = jnp.einsum("mhsd,de->mhse", tokens, triple[0], precision=HIGH)
    keys_all = jnp.einsum("mhsd,de->mhse", tokens, triple[1], precision=HIGH)
    values = jnp.einsum("mhsd,de->mhse", tokens, triple[2], precision=HIGH)
    scores = jnp.einsum("mhsd,mhtd->mhst", queries, keys_all, precision=HIGH) * DH ** (-0.5)
    return jnp.einsum("mhst,mhtd->mhsd", jax.nn.softmax(scores, axis=-1), values, precision=HIGH)


def out_piece(hidden, weights, mixed, matrices, packed, layer_index, onehot):
    vectors = unpack(packed)["vec"][layer_index]
    points = hidden.shape[0]
    spread_wts = onehot[:, :, None, None] * weights[:, None, :, :]
    pointwise = jnp.einsum("pmhs,mhsd->phd", spread_wts, mixed, precision=HIGH).reshape(points, C)
    hidden = hidden + matmul(pointwise, matrices[2]) + vectors[4]
    normed = norm_rows(hidden, vectors[5], vectors[6])
    inner = jax.nn.gelu(matmul(normed, matrices[3]) + vectors[7], approximate=False)
    return hidden + matmul(inner, matrices[4]) + vectors[8]


def head_piece(hidden, packed, target, onehot):
    params = unpack(packed)
    normed = norm_rows(hidden, params["fin"][0], params["fin"][1])
    predicted = matmul(normed, params["head_w"]) + params["head_b"]
    misfit = predicted - target
    errors = matmul(onehot.T, jnp.sum(misfit * misfit, axis=-1))
    scales = matmul(onehot.T, jnp.sum(target * target, axis=-1))
    return (errors, scales)


def loss_piece(errors, scales, meshes, floor_value):
    return jnp.sum(jnp.sqrt((errors + 1e-06) / jnp.maximum(scales, floor_value))) / meshes


def one_cycle(count):
    start_rate = peak_rate / 25.0
    end_rate = start_rate / 10000.0
    rising = start_rate + (peak_rate - start_rate) * 0.5 * (
        1.0 - jnp.cos(math.pi * count / warm_steps)
    )
    falling = end_rate + (peak_rate - end_rate) * 0.5 * (
        1.0 + jnp.cos(math.pi * (count - warm_steps) / (total_steps - warm_steps))
    )
    return jnp.where(count <= warm_steps, rising, falling)


def newton_schulz(current, gram_of):
    for sweep in range(5):
        gram = gram_of(current)
        product = jnp.einsum("...rc,...cd->...rd", current, gram, precision=HIGH)
        current = (
            ns_a * current
            + ns_b * product
            + ns_c * jnp.einsum("...rc,...cd->...rd", product, gram, precision=HIGH)
        )
    return current


def apply_update(
    grad_muon,
    grad_adam,
    square_sum,
    step_count,
    muon_weight,
    muon_moment,
    adam_weight,
    adam_first,
    adam_second,
    frob_of,
    orthogonal_of,
):
    norm_value = jnp.sqrt(square_sum)
    factor = 0.1 / jnp.maximum(norm_value, 0.1)
    moment = 0.95 * muon_moment + factor * grad_muon
    normalized = moment / (jnp.sqrt(frob_of(moment)) + 1e-07)[..., None, None]
    current = orthogonal_of(normalized)
    count = step_count[0].astype(jnp.float32)
    rate = one_cycle(count)
    new_muon = muon_weight * (1.0 - rate * 0.01) - rate * (0.2 * C**0.5) * current
    clipped = factor * grad_adam
    first = 0.9 * adam_first + 0.1 * clipped
    second = 0.999 * adam_second + 0.001 * clipped * clipped
    first_hat = first / (1.0 - 0.9**count)
    second_hat = second / (1.0 - 0.999**count)
    new_adam = adam_weight * (1.0 - rate * 0.01) - rate * first_hat / (jnp.sqrt(second_hat) + 1e-08)
    return (new_muon, moment, new_adam, first, second, norm_value)


def local(
    inputs,
    target,
    lengths,
    step_count,
    muon_weight,
    muon_moment,
    adam_weight,
    adam_first,
    adam_second,
):
    muon_all, adam_all = (
        lax.all_gather(muon_weight, ("mesh", "pts"), axis=2, tiled=True),
        lax.all_gather(adam_weight, ("mesh", "pts"), axis=0, tiled=True),
    )
    points = inputs.shape[0]
    pts_count = lax.axis_size("pts")
    floor_value = float(points * pts_count)
    onehot = mesh_mask(lengths[0], lax.axis_index("pts") * points, points)
    meshes = lax.axis_size("mesh") * lengths.shape[1]
    hidden, embed_back = jax.vjp(lambda packed: embed_piece(inputs, packed), adam_all)
    saved = []
    for layer_index in range(L):
        matrices = muon_all[layer_index]
        (weights, numerator, denominator), slice_back = jax.vjp(
            partial(slice_piece, layer_index=layer_index, onehot=onehot), hidden, matrices, adam_all
        )
        numerator, denominator = lax.psum((numerator, denominator), "pts")
        mixed, mix_back = jax.vjp(
            partial(mix_piece, layer_index=layer_index), numerator, denominator, adam_all
        )
        following, out_back = jax.vjp(
            partial(out_piece, layer_index=layer_index, onehot=onehot),
            hidden,
            weights,
            mixed,
            matrices,
            adam_all,
        )
        saved.append((slice_back, mix_back, out_back))
        hidden = following
    (errors, scales), head_back = jax.vjp(
        lambda state, packed: head_piece(state, packed, target, onehot), hidden, adam_all
    )
    errors, scales = lax.psum((errors, scales), "pts")
    group_loss, loss_back = jax.vjp(
        lambda first, second: loss_piece(first, second, meshes, floor_value), errors, scales
    )
    grad_errors, grad_scales = loss_back(jnp.ones_like(group_loss))
    grad_hidden, grad_adam = head_back((grad_errors, grad_scales))
    grad_layers = [None] * L
    for layer_index in reversed(range(L)):
        slice_back, mix_back, out_back = saved[layer_index]
        grad_hidden_out, grad_weights, grad_mixed, grad_mats_out, grad_adam_out = out_back(
            grad_hidden
        )
        grad_mixed = lax.psum(grad_mixed, "pts")
        grad_num, grad_den, grad_adam_mix = mix_back(grad_mixed)
        grad_hidden_in, grad_mats_in, grad_adam_in = slice_back((grad_weights, grad_num, grad_den))
        grad_hidden = grad_hidden_out + grad_hidden_in
        grad_adam = grad_adam + grad_adam_out + grad_adam_in + grad_adam_mix / pts_count
        grad_layers[layer_index] = grad_mats_out + grad_mats_in
    (grad_embed,) = embed_back(grad_hidden)
    grad_adam = grad_adam + grad_embed
    grad_muon = jnp.stack(grad_layers)
    grad_muon, grad_adam = (
        lax.psum_scatter(grad_muon, ("mesh", "pts"), scatter_dimension=2, tiled=True),
        lax.psum_scatter(grad_adam, ("mesh", "pts"), scatter_dimension=0, tiled=True),
    )
    square_sum, loss_total = lax.psum(
        (jnp.sum(grad_muon * grad_muon) + jnp.sum(grad_adam * grad_adam), group_loss / pts_count),
        ("mesh", "pts"),
    )

    def frob_of(moment):
        return lax.psum(jnp.sum(moment * moment, axis=(2, 3)), ("mesh", "pts"))

    def orthogonal_of(normalized):
        groups = lax.axis_size("mesh")
        count_all = normalized.shape[0] * normalized.shape[1]
        per_group = (count_all + groups - 1) // groups
        stacked = normalized.reshape((count_all,) + normalized.shape[2:])
        filler = jnp.zeros((per_group * groups - count_all,) + normalized.shape[2:], jnp.float32)
        spread = lax.all_to_all(
            jnp.concatenate([stacked, filler], axis=0),
            "mesh",
            split_axis=0,
            concat_axis=1,
            tiled=True,
        )

        def gram_of(current):
            return lax.psum(jnp.einsum("krc,krd->kcd", current, current, precision=HIGH), "pts")

        finished = newton_schulz(spread, gram_of)
        returned = lax.all_to_all(finished, "mesh", split_axis=1, concat_axis=0, tiled=True)
        return returned[:count_all].reshape(normalized.shape)

    results = apply_update(
        grad_muon,
        grad_adam,
        square_sum,
        step_count,
        muon_weight,
        muon_moment,
        adam_weight,
        adam_first,
        adam_second,
        frob_of,
        orthogonal_of,
    )
    return (results[0], results[1], results[2], results[3], results[4], loss_total, results[5])


def solution(mesh):
    in_specs = (
        P(("mesh", "pts"), None),
        P(("mesh", "pts"), None),
        P("mesh", None),
        P(),
        P(None, None, ("mesh", "pts"), None),
        P(None, None, ("mesh", "pts"), None),
        P(("mesh", "pts")),
        P(("mesh", "pts")),
        P(("mesh", "pts")),
    )
    out_specs = (
        P(None, None, ("mesh", "pts"), None),
        P(None, None, ("mesh", "pts"), None),
        P(("mesh", "pts")),
        P(("mesh", "pts")),
        P(("mesh", "pts")),
        P(),
        P(),
    )
    return jax.shard_map(local, mesh=mesh, in_specs=in_specs, out_specs=out_specs, check_vma=False)
```

profile of v0, /device:TPU:0, one launch (start us, length us, event | category | flops | bytes accessed | tf_op | source)
XLA Modules:
  0.0 1215.2 jit_solution(13003831298324453706)
XLA Ops:
  12.7 125.0 %all-reduce.100.cloned.1.call-done = f32[18848]{0:T(1024)} async-done(((f32[18848]{0:T(1024)}), f32[18848]{0:T(1024)}) %all-reduce.100.cloned.1.call-update) | async-done | bytes 75408
  154.3 45.1 %all-gather.2.cloned.1.call-done = f32[2,5,256,256]{3,2,1,0:T(8,128)} async-done(((f32[2,5,8,256]{3,2,1,0:T(8,128)}), f32[2,5,256,256]{3,2,1,0:T(8,128)}) %all-gather.2.cloned.1.call-update) | async-done | bytes 2621456 | tf_op jit(solution)/shard_map/all_gather | solution.py:191
  199.5 2.3 convolution_add_fusion.11
  201.8 2.1 fusion.227
  206.6 11.4 psum.113
  219.3 2.3 convolution_add_fusion.12
  222.5 4.7 fusion.42
  229.9 29.6 %all-reduce.82.cloned.1.call-done = f32[4,8,64,32]{2,3,0,1:T(8,128)} async-done(((f32[4,8,64,32]{2,3,0,1:T(8,128)}), f32[4,8,64,32]{2,3,0,1:T(8,128)}) %all-reduce.82.cloned.1.call-update) | async-done | bytes 262160 | tf_op jit(solution)/shard_map/psum | solution.py:206
  267.9 5.2 fusion.2
  273.2 2.4 fusion.246
  275.8 5.3 fusion.58
  281.2 2.4 fusion.247
  283.8 2.3 convolution_add_fusion.6
  291.5 10.1 psum.115
  302.9 2.3 convolution_add_fusion.7
  306.2 4.7 fusion.47
  311.7 33.0 %all-reduce.84.cloned.1.call-done = f32[4,8,64,32]{2,3,0,1:T(8,128)} async-done(((f32[4,8,64,32]{2,3,0,1:T(8,128)}), f32[4,8,64,32]{2,3,0,1:T(8,128)}) %all-reduce.84.cloned.1.call-update) | async-done | bytes 262160 | tf_op jit(solution)/shard_map/psum | solution.py:206
  353.5 5.2 fusion
  358.8 2.3 fusion.249
  361.3 5.4 fusion.59
  366.8 2.4 fusion.250
  372.0 5.7 all-reduce.69
  377.9 2.9 fusion.72
  380.8 2.6 fusion.257
  383.4 2.5 copy.283
  386.0 2.6 multiply_reduce_fusion.11
  390.5 2.6 convolution_bitcast_fusion.6
  393.0 3.7 fusion.256
  398.7 3.5 fusion.255
  402.2 2.6 copy.284
  412.6 12.3 %fusion.40 = f32[4,8,64,32]{2,3,0,1:T(8,128)} fusion(f32[8,32,1024,1]{2,1,3,0:T(8,128)S(1)} %convolution_bitcast_fusion.1, f32[1024,8,64]{0,2,1:T(8,128)S(1)} %copy-done.16, f32[1024,4]{0,1:T(4,128)S(1)} %copy-done.107), kind=kOutput, calls=%fused_computation.83 | convolution fusion | flops 807403520 | bytes 3424256 | tf_op jit(solution)/shard_map/transpose(jvp(pmhs,mhsd->phd))/dot_general | solution.py:104
  424.8 10.0 multiply_reduce_fusion.1
  444.8 23.6 %all-reduce.86.cloned.1.call-done = f32[4,8,64,32]{2,3,0,1:T(8,128)} async-done(((f32[4,8,64,32]{2,3,0,1:T(8,128)}), f32[4,8,64,32]{2,3,0,1:T(8,128)}) %all-reduce.86.cloned.1.call-update) | async-done | bytes 262160 | tf_op jit(solution)/shard_map/psum | solution.py:235
  468.5 3.6 multiply_reduce_fusion.15
  480.6 4.8 fusion.13
  485.5 3.4 multiply_reduce_fusion.5
  490.8 2.4 convolution_bitcast_fusion.19
  493.2 2.9 fusion.254
  498.0 3.2 convolution_bitcast_fusion.2
  505.1 3.1 fusion.229
  510.9 2.6 convolution_bitcast_fusion.11
  513.5 3.6 fusion.253
  519.1 3.6 fusion.252
  529.0 12.6 %fusion.41 = f32[4,8,64,32]{2,3,0,1:T(8,128)} fusion(f32[8,32,1024,1]{2,1,3,0:T(8,128)S(1)} %convolution_bitcast_fusion, f32[1024,8,64]{0,2,1:T(8,128)S(1)} %copy-done.9, f32[1024,4]{0,1:T(4,128)S(1)} %copy-done.109), kind=kOutput, calls=%fused_computation.84 | convolution fusion | flops 807403520 | bytes 3424256 | tf_op jit(solution)/shard_map/transpose(jvp(pmhs,mhsd->phd))/dot_general | solution.py:104
  541.7 9.7 multiply_reduce_fusion
  570.0 3.0 convolution_bitcast_fusion.9
  572.9 30.5 %all-reduce.88.cloned.1.call-done = f32[4,8,64,32]{2,3,0,1:T(8,128)} async-done(((f32[4,8,64,32]{2,3,0,1:T(8,128)}), f32[4,8,64,32]{2,3,0,1:T(8,128)}) %all-reduce.88.cloned.1.call-update) | async-done | bytes 262160 | tf_op jit(solution)/shard_map/psum | solution.py:235
  603.5 3.2 multiply_reduce_fusion.12
  615.2 4.0 fusion.12
  619.2 3.5 multiply_reduce_fusion.4
  626.3 2.3 fusion.251
  634.5 2.9 multiply_reduce_fusion.7
  647.5 117.7 %all-reduce.102.cloned.1.call-done = f32[18848]{0:T(1024)} async-done(((f32[18848]{0:T(1024)}), f32[18848]{0:T(1024)}) %all-reduce.102.cloned.1.call-update) | async-done | bytes 75408
  766.6 142.6 %reduce-scatter.2.cloned.1.call-done = f32[2,5,8,256]{3,2,1,0:T(8,128)} async-done(((f32[2,5,256,256]{3,2,1,0:T(8,128)}), f32[2,5,8,256]{3,2,1,0:T(8,128)}) %reduce-scatter.2.cloned.1.call-update) | async-done | bytes 81936 | tf_op jit(solution)/shard_map/reduce_scatter | solution.py:245
  912.6 36.8 %psum.120 = f32[]{:T(128)} all-reduce(f32[]{:T(128)S(6)} %add.556), channel_id=1, replica_groups=mesh['mesh'=8,'pts'=4] {'mesh','pts'}, use_global_device_ids=true, to_apply=%region_77.78 | all-reduce | flops 1 | bytes 8 | tf_op jit(solution)/shard_map/psum | solution.py:248
  951.2 41.2 %all-reduce.68 = (f32[2,5]{1,0:T(2,128)S(1)}, f32[]{:T(128)}) all-reduce(f32[2,5]{1,0:T(2,128)S(1)} %get-tuple-element.29, f32[]{:T(128)S(6)} %div.387), channel_id=1, replica_groups=mesh['mesh'=8,'pts'=4] {'mesh','pts'}, use_global_device_ids=true, to_apply=%region_79.80 | all-reduce | flops 11 | bytes 88 | tf_op jit(solution)/shard_map/psum | solution.py:254
  992.5 11.9 all_to_all.33
  1005.9 31.6 %all-reduce.90.cloned.1.call-done = f32[2,256,256]{2,1,0:T(8,128)} async-done(((f32[2,256,256]{2,1,0:T(8,128)}), f32[2,256,256]{2,1,0:T(8,128)}) %all-reduce.90.cloned.1.call-update) | async-done | bytes 524304 | tf_op jit(solution)/shard_map/psum | solution.py:271
  1042.1 33.6 %all-reduce.92.cloned.1.call-done = f32[2,256,256]{2,1,0:T(8,128)} async-done(((f32[2,256,256]{2,1,0:T(8,128)}), f32[2,256,256]{2,1,0:T(8,128)}) %all-reduce.92.cloned.1.call-update) | async-done | bytes 524304 | tf_op jit(solution)/shard_map/psum | solution.py:271
  1080.2 33.6 %all-reduce.94.cloned.1.call-done = f32[2,256,256]{2,1,0:T(8,128)} async-done(((f32[2,256,256]{2,1,0:T(8,128)}), f32[2,256,256]{2,1,0:T(8,128)}) %all-reduce.94.cloned.1.call-update) | async-done | bytes 524304 | tf_op jit(solution)/shard_map/psum | solution.py:271
  1118.5 33.4 %all-reduce.96.cloned.1.call-done = f32[2,256,256]{2,1,0:T(8,128)} async-done(((f32[2,256,256]{2,1,0:T(8,128)}), f32[2,256,256]{2,1,0:T(8,128)}) %all-reduce.96.cloned.1.call-update) | async-done | bytes 524304 | tf_op jit(solution)/shard_map/psum | solution.py:271
  1156.4 33.7 %all-reduce.98.cloned.1.call-done = f32[2,256,256]{2,1,0:T(8,128)} async-done(((f32[2,256,256]{2,1,0:T(8,128)}), f32[2,256,256]{2,1,0:T(8,128)}) %all-reduce.98.cloned.1.call-update) | async-done | bytes 524304 | tf_op jit(solution)/shard_map/psum | solution.py:271
  1193.8 5.5 all-to-all-start.1
  1201.7 5.0 all-to-all-done.1
  (684 shorter events, 182.0 us)
Async XLA Ops:
  7.2 141.5 %copy-start = (f32[1024,8]{0,1:T(8,128)S(1)}, f32[1024,8]{0,1:T(8,128)}, u32[]{:S(2)}) copy-start(f32[1024,8]{0,1:T(8,128)} %param.9) | copy-start | bytes 98308
  7.2 130.6 %all-reduce.100.cloned.1.call-start = ((), (), s32[]{:S(2)}) async-start(), calls=%async_computation.14 | async-start | bytes 155648
  8.8 190.7 %all-gather.2.cloned.1.call-start = ((), (), s32[]{:S(2)}) async-start(), calls=%async_computation.3 | async-start | bytes 2703360 | tf_op jit(solution)/shard_map/all_gather | solution.py:191
  9.6 250.0 %all-reduce.82.cloned.1.call-start = ((), (), s32[]{:S(2)}) async-start(), calls=%async_computation.4 | async-start | bytes 1048576 | tf_op jit(solution)/shard_map/psum | solution.py:206
  10.4 279.7 %copy-start.153 = (s32[4,1]{0,1:T(1,128)}, s32[4,1]{0,1:T(1,128)S(1)}, u32[]{:S(2)}) copy-start(s32[4,1]{0,1:T(1,128)S(1)} %reduce-window.4) | copy-start | bytes 52
  11.8 278.3 %copy-start.156 = (s32[4]{0:T(128)}, s32[4]{0:T(128)S(1)}, u32[]{:S(2)}) copy-start(s32[4]{0:T(128)S(1)} %fusion.197) | copy-start | bytes 52
  11.9 189.8 %copy-start.192 = (pred[4,1024]{1,0:T(4,128)(4,1)}, pred[4,1024]{1,0:T(4,128)(4,1)S(1)}, u32[]{:S(2)}) copy-start(pred[4,1024]{1,0:T(4,128)(4,1)S(1)} %compare_and_fusion) | copy-start | bytes 12292
  12.7 340.4 %copy-start.106 = (f32[1024,4]{0,1:T(4,128)}, f32[1024,4]{0,1:T(4,128)S(1)}, u32[]{:S(2)}) copy-start(f32[1024,4]{0,1:T(4,128)S(1)} %fusion.222) | copy-start | bytes 49156
  146.4 139.7 %copy-start.129 = (f32[32,64,1]{1,0,2:T(8,128)}, f32[32,64,1]{1,0,2:T(8,128)S(1)}, u32[]{:S(2)}) copy-start(f32[32,64,1]{1,0,2:T(8,128)S(1)} %reshape.745) | copy-start | bytes 24580
  146.5 55.3 %copy-start.124 = (f32[32,64,1]{1,0,2:T(8,128)}, f32[32,64,1]{1,0,2:T(8,128)S(1)}, u32[]{:S(2)}) copy-start(f32[32,64,1]{1,0,2:T(8,128)S(1)} %reshape.738) | copy-start | bytes 24580
  148.6 70.6 %copy-start.137 = (f32[256]{0:T(256)}, f32[256]{0:T(256)S(1)}, u32[]{:S(2)}) copy-start(f32[256]{0:T(256)S(1)} %get-tuple-element.83) | copy-start | bytes 3076
  149.8 54.1 %copy-start.139 = (f32[1024]{0:T(1024)}, f32[1024]{0:T(1024)S(1)}, u32[]{:S(2)}) copy-start(f32[1024]{0:T(1024)S(1)} %multiply_reduce_fusion.22) | copy-start | bytes 12292
  151.2 53.2 %copy-start.175 = (f32[64]{0:T(128)}, f32[64]{0:T(128)S(1)}, u32[]{:S(2)}) copy-start(f32[64]{0:T(128)S(1)} %get-tuple-element.79) | copy-start | bytes 772
  152.6 51.9 %copy-start.177 = (f32[8]{0:T(128)}, f32[8]{0:T(128)S(1)}, u32[]{:S(2)}) copy-start(f32[8]{0:T(128)S(1)} %get-tuple-element.51) | copy-start | bytes 100
  154.3 65.0 %copy-start.147 = (f32[256]{0:T(256)}, f32[256]{0:T(256)S(1)}, u32[]{:S(2)}) copy-start(f32[256]{0:T(256)S(1)} %get-tuple-element.70) | copy-start | bytes 3076
  154.3 121.5 %copy-start.151 = (f32[256]{0:T(256)}, f32[256]{0:T(256)S(1)}, u32[]{:S(2)}) copy-start(f32[256]{0:T(256)S(1)} %get-tuple-element.66) | copy-start | bytes 3076
  154.3 148.6 %copy-start.135 = (f32[256]{0:T(256)}, f32[256]{0:T(256)S(1)}, u32[]{:S(2)}) copy-start(f32[256]{0:T(256)S(1)} %get-tuple-element.62) | copy-start | bytes 3076
  154.3 148.6 %copy-start.149 = (f32[256]{0:T(256)}, f32[256]{0:T(256)S(1)}, u32[]{:S(2)}) copy-start(f32[256]{0:T(256)S(1)} %get-tuple-element.61) | copy-start | bytes 3076
  205.3 62.6 %copy-start.8 = (f32[1024,8,64]{0,2,1:T(8,128)}, f32[1024,8,64]{0,2,1:T(8,128)S(1)}, u32[]{:S(2)}) copy-start(f32[1024,8,64]{0,2,1:T(8,128)S(1)} %fusion.36) | copy-start | bytes 6291460
  218.7 46.5 %copy-start.167 = (f32[4,8,64]{2,0,1:T(4,128)}, f32[4,8,64]{2,0,1:T(4,128)S(1)}, u32[]{:S(2)}) copy-start(f32[4,8,64]{2,0,1:T(4,128)S(1)} %copy.263) | copy-start | bytes 24580
  227.2 34.0 %copy-start.166 = (f32[32,32]{1,0:T(8,128)S(1)}, f32[32,32]{1,0:T(8,128)}, u32[]{:S(2)}) copy-start(f32[32,32]{1,0:T(8,128)} %squeeze.71) | copy-start | bytes 12292
  227.2 117.4 %all-reduce.84.cloned.1.call-start = ((), (), s32[]{:S(2)}) async-start(), calls=%async_computation.5 | async-start | bytes 1048576 | tf_op jit(solution)/shard_map/psum | solution.py:206
  265.2 45.9 %copy-start.127 = (f32[4,8,64]{2,1,0:T(8,128)}, f32[4,8,64]{2,1,0:T(8,128)S(1)}, u32[]{:S(2)}) copy-start(f32[4,8,64]{2,1,0:T(8,128)S(1)} %fusion.85) | copy-start | bytes 24580
  267.9 5.2 copy-start.186
  275.6 5.5 copy-start.104
  275.7 5.4 copy-start.141
  275.8 5.3 copy-start.115
  275.8 5.3 copy-start.198
  283.8 19.1 %copy-start.98 = (f32[1024]{0:T(1024)}, f32[1024]{0:T(1024)S(1)}, u32[]{:S(2)}) copy-start(f32[1024]{0:T(1024)S(1)} %fusion.194) | copy-start | bytes 12292
  290.2 12.7 %copy-start.184 = (f32[256]{0:T(256)S(1)}, f32[256]{0:T(256)}, u32[]{:S(2)}) copy-start(f32[256]{0:T(256)} %get-tuple-element.60) | copy-start | bytes 3076
  302.3 48.1 %copy-start.170 = (f32[4,8,64]{2,0,1:T(4,128)}, f32[4,8,64]{2,0,1:T(4,128)S(1)}, u32[]{:S(2)}) copy-start(f32[4,8,64]{2,0,1:T(4,128)S(1)} %copy.273) | copy-start | bytes 24580
  306.2 38.5 %copy-start.164 = (f32[32,32]{1,0:T(8,128)S(1)}, f32[32,32]{1,0:T(8,128)}, u32[]{:S(2)}) copy-start(f32[32,32]{1,0:T(8,128)} %squeeze.81) | copy-start | bytes 12292
  310.8 35.5 %copy-start.165 = (f32[32,32]{1,0:T(8,128)S(1)}, f32[32,32]{1,0:T(8,128)}, u32[]{:S(2)}) copy-start(f32[32,32]{1,0:T(8,128)} %squeeze.80) | copy-start | bytes 12292
  310.9 157.6 %all-reduce.86.cloned.1.call-start = ((), (), s32[]{:S(2)}) async-start(), calls=%async_computation.6 | async-start | bytes 1048576 | tf_op jit(solution)/shard_map/psum | solution.py:235
  350.4 20.9 %copy-start.132 = (f32[4,8,64]{2,1,0:T(8,128)}, f32[4,8,64]{2,1,0:T(8,128)S(1)}, u32[]{:S(2)}) copy-start(f32[4,8,64]{2,1,0:T(8,128)S(1)} %fusion.87) | copy-start | bytes 24580
  361.1 5.7 copy-start.1
  361.3 5.5 copy-start.197
  371.2 14.8 %copy-start.110 = (f32[1024,4]{0,1:T(4,128)}, f32[1024,4]{0,1:T(4,128)S(1)}, u32[]{:S(2)}) copy-start(f32[1024,4]{0,1:T(4,128)S(1)} %get-tuple-element.114) | copy-start | bytes 49156
  377.7 8.3 copy-start.211
  377.7 8.3 copy-start.213
  377.9 8.1 copy-start.162
  388.9 7.8 copy-start.27
  434.8 168.6 %all-reduce.88.cloned.1.call-start = ((), (), s32[]{:S(2)}) async-start(), calls=%async_computation.7 | async-start | bytes 1048576 | tf_op jit(solution)/shard_map/psum | solution.py:235
  479.4 6.0 copy-start.217
  510.4 6.7 copy-start.29
  541.7 9.7 copy-start.161
  541.7 10.3 copy-start.171
  553.8 12.6 %copy-start.160 = (f32[8,32]{1,0:T(8,128)S(1)}, f32[8,32]{1,0:T(8,128)}, u32[]{:S(2)}) copy-start(f32[8,32]{1,0:T(8,128)} %get-tuple-element.135) | copy-start | bytes 3076
  556.2 47.2 %copy-start.23 = (f32[4,8,64,64]{2,3,1,0:T(8,128)S(1)}, f32[4,8,64,64]{2,3,1,0:T(8,128)}, u32[]{:S(2)}) copy-start(f32[4,8,64,64]{2,3,1,0:T(8,128)} %copy-done.22) | copy-start | bytes 1572868
  556.2 47.2 %copy-start.101 = (f32[4,8,64]{2,1,0:T(8,128)S(1)}, f32[4,8,64]{2,1,0:T(8,128)}, u32[]{:S(2)}) copy-start(f32[4,8,64]{2,1,0:T(8,128)} %copy-done.100) | copy-start | bytes 24580
  569.8 195.4 %all-reduce.102.cloned.1.call-start = ((), (), s32[]{:S(2)}) async-start(), calls=%async_computation.15 | async-start | bytes 155648
  644.0 265.1 %reduce-scatter.2.cloned.1.call-start = ((), (), s32[]{:S(2)}) async-start(), calls=%async_computation.8 | async-start | bytes 2703360 | tf_op jit(solution)/shard_map/reduce_scatter | solution.py:245
  646.2 304.0 %copy-start.114 = (f32[2,5,8,256]{3,2,1,0:T(8,128)S(1)}, f32[2,5,8,256]{3,2,1,0:T(8,128)}, u32[]{:S(2)}) copy-start(f32[2,5,8,256]{3,2,1,0:T(8,128)} %param.14) | copy-start | bytes 245764
  646.3 391.3 %all-reduce.90.cloned.1.call-start = ((), (), s32[]{:S(2)}) async-start(), calls=%async_computation.9 | async-start | bytes 1048576 | tf_op jit(solution)/shard_map/psum | solution.py:271
  951.2 90.8 %copy-start.93 = (f32[2,5,8,256]{3,2,1,0:T(8,128)}, f32[2,5,8,256]{3,2,1,0:T(8,128)S(1)}, u32[]{:S(2)}) copy-start(f32[2,5,8,256]{3,2,1,0:T(8,128)S(1)} %get-tuple-element.30) | copy-start | bytes 245764
  1005.9 69.8 %all-reduce.92.cloned.1.call-start = ((), (), s32[]{:S(2)}) async-start(), calls=%async_computation.10 | async-start | bytes 1048576 | tf_op jit(solution)/shard_map/psum | solution.py:271
  1042.0 71.8 %all-reduce.94.cloned.1.call-start = ((), (), s32[]{:S(2)}) async-start(), calls=%async_computation.11 | async-start | bytes 1048576 | tf_op jit(solution)/shard_map/psum | solution.py:271
  1080.1 71.8 %all-reduce.96.cloned.1.call-start = ((), (), s32[]{:S(2)}) async-start(), calls=%async_computation.12 | async-start | bytes 1048576 | tf_op jit(solution)/shard_map/psum | solution.py:271
  1118.2 71.9 %all-reduce.98.cloned.1.call-start = ((), (), s32[]{:S(2)}) async-start(), calls=%async_computation.13 | async-start | bytes 1048576 | tf_op jit(solution)/shard_map/psum | solution.py:271
  1153.4 46.9 %copy-start.173 = (f32[589]{0:T(1024)S(1)}, f32[589]{0:T(1024)}, u32[]{:S(2)}) copy-start(f32[589]{0:T(1024)} %param.15) | copy-start | bytes 7072
  1153.4 46.9 %copy-start.194 = (f32[589]{0:T(1024)S(1)}, f32[589]{0:T(1024)}, u32[]{:S(2)}) copy-start(f32[589]{0:T(1024)} %param.16) | copy-start | bytes 7072
  1153.4 46.9 %copy-start.195 = (f32[589]{0:T(1024)S(1)}, f32[589]{0:T(1024)}, u32[]{:S(2)}) copy-start(f32[589]{0:T(1024)} %param.17) | copy-start | bytes 7072
  1154.9 51.8 %copy-start.94 = (f32[2,5,8,256]{3,2,1,0:T(8,128)S(1)}, f32[2,5,8,256]{3,2,1,0:T(8,128)}, u32[]{:S(2)}) copy-start(f32[2,5,8,256]{3,2,1,0:T(8,128)} %param.13) | copy-start | bytes 245764
  1193.8 12.9 %all-to-all-start.1 = ((f32[2,64,256]{2,0,1:T(2,128)}), f32[2,64,256]{2,0,1:T(2,128)S(1)}, u32[]{:S(2)}, u32[]{:S(2)}) async-start(f32[2,64,256]{2,0,1:T(2,128)} %copy.325), calls=%async_computation.2 | async-start | bytes 262144 | tf_op jit(solution)/shard_map/all_to_all | solution.py:274
  (170 other events, 471.4 us)
Sparse Core Ops, SparseCore 0:
  14.1 123.5 all-reduce.99
  140.6 58.7 all-gather.1
  227.3 32.1 all-reduce.81
  311.0 33.6 all-reduce.83
  435.0 33.4 all-reduce.85
  569.9 33.5 all-reduce.87
  644.2 120.9 all-reduce.101
  767.5 141.6 reduce-scatter.1
  1006.0 31.5 all-reduce.89
  1042.1 33.4 all-reduce.91
  1080.3 33.4 all-reduce.93
  1118.4 33.4 all-reduce.95
  1156.5 33.5 all-reduce.97
where the time goes:
time: 1220 us
  waiting for transfers between devices  719 us (59%)
  matrix products  250 us (20%)
  blocking collectives  117 us (10%)
  local copies, waits for them, and re-layouts  57.1 us (5%)
  other arithmetic  42.7 us (4%)
  between operations  22.1 us (2%)
    unnamed x15, waiting for transfers between devices  244 us
    psum x5, waiting for transfers between devices, gram_of(): lax.psum(jnp.einsum('krc,krd->kcd', current, current, precision=HIGH), 'p...  166 us
    reduce_scatter x1, waiting for transfers between devices, local(): lax.psum_scatter(grad_muon, ('mesh', 'pts'), scatter_dimension=2, tiled=T...  143 us
    dot_general x38, matrix products, matmul(): return jnp.dot(left, right, precision=HIGH)  87 us
    psum x2, waiting for transfers between devices, local(): numerator, denominator = lax.psum((numerator, denominator), 'pts')  62.6 us
    dot_general x6, matrix products, out_piece(): jnp.einsum('pmhs,mhsd->phd', spread_wts, mixed, precision=HIGH)  54.9 us
    psum x2, waiting for transfers between devices, local(): grad_mixed = lax.psum(grad_mixed, 'pts')  54.1 us
    all_gather x1, waiting for transfers between devices, local(): lax.all_gather(muon_weight, ('mesh', 'pts'), axis=2, tiled=True)  45.1 us
  transfers between devices with their start and end apart: 14, of which 14 were waited for; matrix products, arithmetic and copies ran while one was open for 3% of the time, Pallas kernels for 0%

commit v1 on v0

--- a/solution.py
+++ b/solution.py
@@ -251,7 +251,9 @@
     )
 
     def frob_of(moment):
-        return lax.psum(jnp.sum(moment * moment, axis=(2, 3)), ("mesh", "pts"))
+        return jnp.sum(
+            lax.all_gather(jnp.sum(moment * moment, axis=(2, 3)), ("mesh", "pts")), axis=0
+        )
 
     def orthogonal_of(normalized):
         groups = lax.axis_size("mesh")

time: 1220 us -> 1220 us (level)
    psum x1 -> x0, blocking collectives: 41.2 us -> none  [frob_of(): return lax.psum(jnp.sum(moment * moment, axis=(2, 3)), ('mesh', 'pts'))]
    all_gather x0 -> x1, blocking collectives: none -> 40 us  [frob_of(): lax.all_gather(jnp.sum(moment * moment, axis=(2, 3)), ('mesh', 'pts'))]
where the time goes in v1:
time: 1220 us; the launch traced here: 1210 us
  waiting for transfers between devices  717 us (59%)
  matrix products  250 us (20%)
  blocking collectives  114 us (9%)
  local copies, waits for them, and re-layouts  57.1 us (5%)
  other arithmetic  42.8 us (4%)
  between operations  22.1 us (2%)
    unnamed x15, waiting for transfers between devices  243 us
    psum x5, waiting for transfers between devices, gram_of(): lax.psum(jnp.einsum('krc,krd->kcd', current, current, precision=HIGH), 'p...  165 us
    reduce_scatter x1, waiting for transfers between devices, local(): lax.psum_scatter(grad_muon, ('mesh', 'pts'), scatter_dimension=2, tiled=T...  143 us
    dot_general x38, matrix products, matmul(): return jnp.dot(left, right, precision=HIGH)  87 us
    psum x2, waiting for transfers between devices, local(): numerator, denominator = lax.psum((numerator, denominator), 'pts')  62.6 us
    dot_general x6, matrix products, out_piece(): jnp.einsum('pmhs,mhsd->phd', spread_wts, mixed, precision=HIGH)  54.9 us
    psum x2, waiting for transfers between devices, local(): grad_mixed = lax.psum(grad_mixed, 'pts')  54.1 us
    all_gather x1, waiting for transfers between devices, local(): lax.all_gather(muon_weight, ('mesh', 'pts'), axis=2, tiled=True)  45.1 us
  transfers between devices with their start and end apart: 14, of which 14 were waited for; matrix products, arithmetic and copies ran while one was open for 3% of the time, Pallas kernels for 0%

profile of v1, /device:TPU:0, one launch (start us, length us, event | category | flops | bytes accessed | tf_op | source)
XLA Modules:
  0.0 1210.9 jit_solution(12038147257246657384)
XLA Ops:
  12.7 125.0 %all-reduce.100.cloned.1.call-done = f32[18848]{0:T(1024)} async-done(((f32[18848]{0:T(1024)}), f32[18848]{0:T(1024)}) %all-reduce.100.cloned.1.call-update) | async-done | bytes 75408
  154.3 45.1 %all-gather.4.cloned.1.call-done = f32[2,5,256,256]{3,2,1,0:T(8,128)} async-done(((f32[2,5,8,256]{3,2,1,0:T(8,128)}), f32[2,5,256,256]{3,2,1,0:T(8,128)}) %all-gather.4.cloned.1.call-update) | async-done | bytes 2621456 | tf_op jit(solution)/shard_map/all_gather | solution.py:191
  199.5 2.3 convolution_add_fusion.11
  201.8 2.1 fusion.227
  206.6 11.4 psum.106
  219.3 2.3 convolution_add_fusion.12
  222.5 4.7 fusion.42
  229.9 29.6 %all-reduce.82.cloned.1.call-done = f32[4,8,64,32]{2,3,0,1:T(8,128)} async-done(((f32[4,8,64,32]{2,3,0,1:T(8,128)}), f32[4,8,64,32]{2,3,0,1:T(8,128)}) %all-reduce.82.cloned.1.call-update) | async-done | bytes 262160 | tf_op jit(solution)/shard_map/psum | solution.py:206
  267.9 5.2 fusion.2
  273.2 2.4 fusion.246
  275.8 5.3 fusion.58
  281.2 2.4 fusion.247
  283.8 2.3 convolution_add_fusion.6
  291.5 10.1 psum.108
  302.9 2.3 convolution_add_fusion.7
  306.2 4.7 fusion.47
  311.7 33.0 %all-reduce.84.cloned.1.call-done = f32[4,8,64,32]{2,3,0,1:T(8,128)} async-done(((f32[4,8,64,32]{2,3,0,1:T(8,128)}), f32[4,8,64,32]{2,3,0,1:T(8,128)}) %all-reduce.84.cloned.1.call-update) | async-done | bytes 262160 | tf_op jit(solution)/shard_map/psum | solution.py:206
  353.5 5.2 fusion
  358.8 2.3 fusion.249
  361.3 5.4 fusion.59
  366.8 2.4 fusion.250
  372.0 5.7 all-reduce.69
  377.9 2.9 fusion.72
  380.8 2.6 fusion.257
  383.4 2.5 copy.283
  386.0 2.6 multiply_reduce_fusion.11
  390.5 2.6 convolution_bitcast_fusion.6
  393.0 3.7 fusion.256
  398.7 3.5 fusion.255
  402.2 2.6 copy.284
  412.6 12.3 %fusion.40 = f32[4,8,64,32]{2,3,0,1:T(8,128)} fusion(f32[8,32,1024,1]{2,1,3,0:T(8,128)S(1)} %convolution_bitcast_fusion.1, f32[1024,8,64]{0,2,1:T(8,128)S(1)} %copy-done.16, f32[1024,4]{0,1:T(4,128)S(1)} %copy-done.107), kind=kOutput, calls=%fused_computation.83 | convolution fusion | flops 807403520 | bytes 3424256 | tf_op jit(solution)/shard_map/transpose(jvp(pmhs,mhsd->phd))/dot_general | solution.py:104
  424.8 10.0 multiply_reduce_fusion.1
  444.8 23.6 %all-reduce.86.cloned.1.call-done = f32[4,8,64,32]{2,3,0,1:T(8,128)} async-done(((f32[4,8,64,32]{2,3,0,1:T(8,128)}), f32[4,8,64,32]{2,3,0,1:T(8,128)}) %all-reduce.86.cloned.1.call-update) | async-done | bytes 262160 | tf_op jit(solution)/shard_map/psum | solution.py:235
  468.5 3.6 multiply_reduce_fusion.15
  480.6 4.8 fusion.13
  485.5 3.4 multiply_reduce_fusion.5
  490.8 2.4 convolution_bitcast_fusion.19
  493.2 2.9 fusion.254
  498.0 3.2 convolution_bitcast_fusion.2
  505.1 3.1 fusion.229
  510.9 2.6 convolution_bitcast_fusion.11
  513.5 3.6 fusion.253
  519.1 3.6 fusion.252
  529.0 12.6 %fusion.41 = f32[4,8,64,32]{2,3,0,1:T(8,128)} fusion(f32[8,32,1024,1]{2,1,3,0:T(8,128)S(1)} %convolution_bitcast_fusion, f32[1024,8,64]{0,2,1:T(8,128)S(1)} %copy-done.9, f32[1024,4]{0,1:T(4,128)S(1)} %copy-done.109), kind=kOutput, calls=%fused_computation.84 | convolution fusion | flops 807403520 | bytes 3424256 | tf_op jit(solution)/shard_map/transpose(jvp(pmhs,mhsd->phd))/dot_general | solution.py:104
  541.7 9.7 multiply_reduce_fusion
  570.0 3.0 convolution_bitcast_fusion.9
  572.9 30.5 %all-reduce.88.cloned.1.call-done = f32[4,8,64,32]{2,3,0,1:T(8,128)} async-done(((f32[4,8,64,32]{2,3,0,1:T(8,128)}), f32[4,8,64,32]{2,3,0,1:T(8,128)}) %all-reduce.88.cloned.1.call-update) | async-done | bytes 262160 | tf_op jit(solution)/shard_map/psum | solution.py:235
  603.5 3.2 multiply_reduce_fusion.12
  615.2 4.0 fusion.12
  619.2 3.5 multiply_reduce_fusion.4
  626.3 2.3 fusion.251
  634.5 2.9 multiply_reduce_fusion.7
  648.2 117.0 %all-reduce.102.cloned.1.call-done = f32[18848]{0:T(1024)} async-done(((f32[18848]{0:T(1024)}), f32[18848]{0:T(1024)}) %all-reduce.102.cloned.1.call-update) | async-done | bytes 75408
  766.6 142.6 %reduce-scatter.2.cloned.1.call-done = f32[2,5,8,256]{3,2,1,0:T(8,128)} async-done(((f32[2,5,256,256]{3,2,1,0:T(8,128)}), f32[2,5,8,256]{3,2,1,0:T(8,128)}) %reduce-scatter.2.cloned.1.call-update) | async-done | bytes 81936 | tf_op jit(solution)/shard_map/reduce_scatter | solution.py:245
  912.0 36.8 %all-reduce.68 = (f32[]{:T(128)}, f32[]{:T(128)}) all-reduce(f32[]{:T(128)S(6)} %add.558, f32[]{:T(128)S(6)} %div.387), channel_id=1, replica_groups=mesh['mesh'=8,'pts'=4] {'mesh','pts'}, use_global_device_ids=true, to_apply=%region_77.78 | all-reduce | flops 2 | bytes 16 | tf_op jit(solution)/shard_map/psum | solution.py:248
  950.6 40.0 %all-gather.1 = f32[32,2,5]{2,1,0:T(2,128)S(1)} all-gather(f32[1,2,5]{2,1,0:T(2,128)S(1)} %bitcast.520), channel_id=2, replica_groups=mesh['mesh'=8,'pts'=4] {'mesh','pts'}, dimensions={0}, use_global_device_ids=true | all-gather | bytes 1320 | tf_op jit(solution)/shard_map/all_gather | solution.py:255
  990.8 10.2 all_to_all.33
  1002.5 30.7 %all-reduce.90.cloned.1.call-done = f32[2,256,256]{2,1,0:T(8,128)} async-done(((f32[2,256,256]{2,1,0:T(8,128)}), f32[2,256,256]{2,1,0:T(8,128)}) %all-reduce.90.cloned.1.call-update) | async-done | bytes 524304 | tf_op jit(solution)/shard_map/psum | solution.py:273
  1037.7 33.6 %all-reduce.92.cloned.1.call-done = f32[2,256,256]{2,1,0:T(8,128)} async-done(((f32[2,256,256]{2,1,0:T(8,128)}), f32[2,256,256]{2,1,0:T(8,128)}) %all-reduce.92.cloned.1.call-update) | async-done | bytes 524304 | tf_op jit(solution)/shard_map/psum | solution.py:273
  1075.8 33.6 %all-reduce.94.cloned.1.call-done = f32[2,256,256]{2,1,0:T(8,128)} async-done(((f32[2,256,256]{2,1,0:T(8,128)}), f32[2,256,256]{2,1,0:T(8,128)}) %all-reduce.94.cloned.1.call-update) | async-done | bytes 524304 | tf_op jit(solution)/shard_map/psum | solution.py:273
  1114.1 33.4 %all-reduce.96.cloned.1.call-done = f32[2,256,256]{2,1,0:T(8,128)} async-done(((f32[2,256,256]{2,1,0:T(8,128)}), f32[2,256,256]{2,1,0:T(8,128)}) %all-reduce.96.cloned.1.call-update) | async-done | bytes 524304 | tf_op jit(solution)/shard_map/psum | solution.py:273
  1152.1 33.7 %all-reduce.98.cloned.1.call-done = f32[2,256,256]{2,1,0:T(8,128)} async-done(((f32[2,256,256]{2,1,0:T(8,128)}), f32[2,256,256]{2,1,0:T(8,128)}) %all-reduce.98.cloned.1.call-update) | async-done | bytes 524304 | tf_op jit(solution)/shard_map/psum | solution.py:273
  1189.5 5.5 all-to-all-start.1
  1197.4 5.0 all-to-all-done.1
  (685 shorter events, 182.1 us)
Async XLA Ops:
  7.2 141.5 %copy-start = (f32[1024,8]{0,1:T(8,128)S(1)}, f32[1024,8]{0,1:T(8,128)}, u32[]{:S(2)}) copy-start(f32[1024,8]{0,1:T(8,128)} %param.9) | copy-start | bytes 98308
  7.2 130.6 %all-reduce.100.cloned.1.call-start = ((), (), s32[]{:S(2)}) async-start(), calls=%async_computation.14 | async-start | bytes 155648
  8.8 190.7 %all-gather.4.cloned.1.call-start = ((), (), s32[]{:S(2)}) async-start(), calls=%async_computation.3 | async-start | bytes 2703360 | tf_op jit(solution)/shard_map/all_gather | solution.py:191
  9.6 250.0 %all-reduce.82.cloned.1.call-start = ((), (), s32[]{:S(2)}) async-start(), calls=%async_computation.4 | async-start | bytes 1048576 | tf_op jit(solution)/shard_map/psum | solution.py:206
  10.4 279.7 %copy-start.153 = (s32[4,1]{0,1:T(1,128)}, s32[4,1]{0,1:T(1,128)S(1)}, u32[]{:S(2)}) copy-start(s32[4,1]{0,1:T(1,128)S(1)} %reduce-window.4) | copy-start | bytes 52
  11.8 278.3 %copy-start.156 = (s32[4]{0:T(128)}, s32[4]{0:T(128)S(1)}, u32[]{:S(2)}) copy-start(s32[4]{0:T(128)S(1)} %fusion.197) | copy-start | bytes 52
  11.9 189.8 %copy-start.192 = (pred[4,1024]{1,0:T(4,128)(4,1)}, pred[4,1024]{1,0:T(4,128)(4,1)S(1)}, u32[]{:S(2)}) copy-start(pred[4,1024]{1,0:T(4,128)(4,1)S(1)} %compare_and_fusion) | copy-start | bytes 12292
  12.7 340.4 %copy-start.106 = (f32[1024,4]{0,1:T(4,128)}, f32[1024,4]{0,1:T(4,128)S(1)}, u32[]{:S(2)}) copy-start(f32[1024,4]{0,1:T(4,128)S(1)} %fusion.222) | copy-start | bytes 49156
  146.4 139.7 %copy-start.129 = (f32[32,64,1]{1,0,2:T(8,128)}, f32[32,64,1]{1,0,2:T(8,128)S(1)}, u32[]{:S(2)}) copy-start(f32[32,64,1]{1,0,2:T(8,128)S(1)} %reshape.752) | copy-start | bytes 24580
  146.5 55.3 %copy-start.124 = (f32[32,64,1]{1,0,2:T(8,128)}, f32[32,64,1]{1,0,2:T(8,128)S(1)}, u32[]{:S(2)}) copy-start(f32[32,64,1]{1,0,2:T(8,128)S(1)} %reshape.745) | copy-start | bytes 24580
  148.6 70.6 %copy-start.137 = (f32[256]{0:T(256)}, f32[256]{0:T(256)S(1)}, u32[]{:S(2)}) copy-start(f32[256]{0:T(256)S(1)} %get-tuple-element.83) | copy-start | bytes 3076
  149.8 54.1 %copy-start.139 = (f32[1024]{0:T(1024)}, f32[1024]{0:T(1024)S(1)}, u32[]{:S(2)}) copy-start(f32[1024]{0:T(1024)S(1)} %multiply_reduce_fusion.22) | copy-start | bytes 12292
  151.2 53.2 %copy-start.175 = (f32[64]{0:T(128)}, f32[64]{0:T(128)S(1)}, u32[]{:S(2)}) copy-start(f32[64]{0:T(128)S(1)} %get-tuple-element.79) | copy-start | bytes 772
  152.6 51.9 %copy-start.177 = (f32[8]{0:T(128)}, f32[8]{0:T(128)S(1)}, u32[]{:S(2)}) copy-start(f32[8]{0:T(128)S(1)} %get-tuple-element.51) | copy-start | bytes 100
  154.3 65.0 %copy-start.147 = (f32[256]{0:T(256)}, f32[256]{0:T(256)S(1)}, u32[]{:S(2)}) copy-start(f32[256]{0:T(256)S(1)} %get-tuple-element.70) | copy-start | bytes 3076
  154.3 121.5 %copy-start.151 = (f32[256]{0:T(256)}, f32[256]{0:T(256)S(1)}, u32[]{:S(2)}) copy-start(f32[256]{0:T(256)S(1)} %get-tuple-element.66) | copy-start | bytes 3076
  154.3 148.6 %copy-start.135 = (f32[256]{0:T(256)}, f32[256]{0:T(256)S(1)}, u32[]{:S(2)}) copy-start(f32[256]{0:T(256)S(1)} %get-tuple-element.62) | copy-start | bytes 3076
  154.3 148.6 %copy-start.149 = (f32[256]{0:T(256)}, f32[256]{0:T(256)S(1)}, u32[]{:S(2)}) copy-start(f32[256]{0:T(256)S(1)} %get-tuple-element.61) | copy-start | bytes 3076
  205.3 62.6 %copy-start.8 = (f32[1024,8,64]{0,2,1:T(8,128)}, f32[1024,8,64]{0,2,1:T(8,128)S(1)}, u32[]{:S(2)}) copy-start(f32[1024,8,64]{0,2,1:T(8,128)S(1)} %fusion.36) | copy-start | bytes 6291460
  218.7 46.5 %copy-start.167 = (f32[4,8,64]{2,0,1:T(4,128)}, f32[4,8,64]{2,0,1:T(4,128)S(1)}, u32[]{:S(2)}) copy-start(f32[4,8,64]{2,0,1:T(4,128)S(1)} %copy.263) | copy-start | bytes 24580
  227.2 34.0 %copy-start.166 = (f32[32,32]{1,0:T(8,128)S(1)}, f32[32,32]{1,0:T(8,128)}, u32[]{:S(2)}) copy-start(f32[32,32]{1,0:T(8,128)} %squeeze.71) | copy-start | bytes 12292
  227.2 117.4 %all-reduce.84.cloned.1.call-start = ((), (), s32[]{:S(2)}) async-start(), calls=%async_computation.5 | async-start | bytes 1048576 | tf_op jit(solution)/shard_map/psum | solution.py:206
  265.2 45.9 %copy-start.127 = (f32[4,8,64]{2,1,0:T(8,128)}, f32[4,8,64]{2,1,0:T(8,128)S(1)}, u32[]{:S(2)}) copy-start(f32[4,8,64]{2,1,0:T(8,128)S(1)} %fusion.85) | copy-start | bytes 24580
  267.9 5.2 copy-start.186
  275.6 5.5 copy-start.104
  275.7 5.4 copy-start.141
  275.8 5.3 copy-start.115
  275.8 5.3 copy-start.198
  283.8 19.1 %copy-start.98 = (f32[1024]{0:T(1024)}, f32[1024]{0:T(1024)S(1)}, u32[]{:S(2)}) copy-start(f32[1024]{0:T(1024)S(1)} %fusion.194) | copy-start | bytes 12292
  290.2 12.7 %copy-start.184 = (f32[256]{0:T(256)S(1)}, f32[256]{0:T(256)}, u32[]{:S(2)}) copy-start(f32[256]{0:T(256)} %get-tuple-element.60) | copy-start | bytes 3076
  302.3 48.1 %copy-start.170 = (f32[4,8,64]{2,0,1:T(4,128)}, f32[4,8,64]{2,0,1:T(4,128)S(1)}, u32[]{:S(2)}) copy-start(f32[4,8,64]{2,0,1:T(4,128)S(1)} %copy.273) | copy-start | bytes 24580
  306.2 38.5 %copy-start.164 = (f32[32,32]{1,0:T(8,128)S(1)}, f32[32,32]{1,0:T(8,128)}, u32[]{:S(2)}) copy-start(f32[32,32]{1,0:T(8,128)} %squeeze.81) | copy-start | bytes 12292
  310.8 35.5 %copy-start.165 = (f32[32,32]{1,0:T(8,128)S(1)}, f32[32,32]{1,0:T(8,128)}, u32[]{:S(2)}) copy-start(f32[32,32]{1,0:T(8,128)} %squeeze.80) | copy-start | bytes 12292
  310.9 157.6 %all-reduce.86.cloned.1.call-start = ((), (), s32[]{:S(2)}) async-start(), calls=%async_computation.6 | async-start | bytes 1048576 | tf_op jit(solution)/shard_map/psum | solution.py:235
  350.4 20.9 %copy-start.132 = (f32[4,8,64]{2,1,0:T(8,128)}, f32[4,8,64]{2,1,0:T(8,128)S(1)}, u32[]{:S(2)}) copy-start(f32[4,8,64]{2,1,0:T(8,128)S(1)} %fusion.87) | copy-start | bytes 24580
  361.1 5.7 copy-start.1
  361.3 5.5 copy-start.197
  371.2 14.8 %copy-start.110 = (f32[1024,4]{0,1:T(4,128)}, f32[1024,4]{0,1:T(4,128)S(1)}, u32[]{:S(2)}) copy-start(f32[1024,4]{0,1:T(4,128)S(1)} %get-tuple-element.114) | copy-start | bytes 49156
  377.7 8.3 copy-start.211
  377.7 8.3 copy-start.213
  377.9 8.1 copy-start.162
  388.9 7.8 copy-start.27
  434.8 168.6 %all-reduce.88.cloned.1.call-start = ((), (), s32[]{:S(2)}) async-start(), calls=%async_computation.7 | async-start | bytes 1048576 | tf_op jit(solution)/shard_map/psum | solution.py:235
  479.4 6.0 copy-start.217
  510.4 6.7 copy-start.29
  541.7 9.7 copy-start.161
  541.7 10.3 copy-start.171
  553.8 12.6 %copy-start.160 = (f32[8,32]{1,0:T(8,128)S(1)}, f32[8,32]{1,0:T(8,128)}, u32[]{:S(2)}) copy-start(f32[8,32]{1,0:T(8,128)} %get-tuple-element.135) | copy-start | bytes 3076
  556.2 47.2 %copy-start.23 = (f32[4,8,64,64]{2,3,1,0:T(8,128)S(1)}, f32[4,8,64,64]{2,3,1,0:T(8,128)}, u32[]{:S(2)}) copy-start(f32[4,8,64,64]{2,3,1,0:T(8,128)} %copy-done.22) | copy-start | bytes 1572868
  556.2 47.2 %copy-start.101 = (f32[4,8,64]{2,1,0:T(8,128)S(1)}, f32[4,8,64]{2,1,0:T(8,128)}, u32[]{:S(2)}) copy-start(f32[4,8,64]{2,1,0:T(8,128)} %copy-done.100) | copy-start | bytes 24580
  569.8 195.4 %all-reduce.102.cloned.1.call-start = ((), (), s32[]{:S(2)}) async-start(), calls=%async_computation.15 | async-start | bytes 155648
  644.0 265.1 %reduce-scatter.2.cloned.1.call-start = ((), (), s32[]{:S(2)}) async-start(), calls=%async_computation.8 | async-start | bytes 2703360 | tf_op jit(solution)/shard_map/reduce_scatter | solution.py:245
  646.2 303.3 %copy-start.114 = (f32[2,5,8,256]{3,2,1,0:T(8,128)S(1)}, f32[2,5,8,256]{3,2,1,0:T(8,128)}, u32[]{:S(2)}) copy-start(f32[2,5,8,256]{3,2,1,0:T(8,128)} %param.14) | copy-start | bytes 245764
  646.3 386.9 %all-reduce.90.cloned.1.call-start = ((), (), s32[]{:S(2)}) async-start(), calls=%async_computation.9 | async-start | bytes 1048576 | tf_op jit(solution)/shard_map/psum | solution.py:273
  950.6 87.0 %copy-start.93 = (f32[2,5,8,256]{3,2,1,0:T(8,128)}, f32[2,5,8,256]{3,2,1,0:T(8,128)S(1)}, u32[]{:S(2)}) copy-start(f32[2,5,8,256]{3,2,1,0:T(8,128)S(1)} %get-tuple-element.30) | copy-start | bytes 245764
  1002.4 68.9 %all-reduce.92.cloned.1.call-start = ((), (), s32[]{:S(2)}) async-start(), calls=%async_computation.10 | async-start | bytes 1048576 | tf_op jit(solution)/shard_map/psum | solution.py:273
  1037.7 71.8 %all-reduce.94.cloned.1.call-start = ((), (), s32[]{:S(2)}) async-start(), calls=%async_computation.11 | async-start | bytes 1048576 | tf_op jit(solution)/shard_map/psum | solution.py:273
  1075.8 71.8 %all-reduce.96.cloned.1.call-start = ((), (), s32[]{:S(2)}) async-start(), calls=%async_computation.12 | async-start | bytes 1048576 | tf_op jit(solution)/shard_map/psum | solution.py:273
  1113.9 71.9 %all-reduce.98.cloned.1.call-start = ((), (), s32[]{:S(2)}) async-start(), calls=%async_computation.13 | async-start | bytes 1048576 | tf_op jit(solution)/shard_map/psum | solution.py:273
  1149.1 46.9 %copy-start.173 = (f32[589]{0:T(1024)S(1)}, f32[589]{0:T(1024)}, u32[]{:S(2)}) copy-start(f32[589]{0:T(1024)} %param.15) | copy-start | bytes 7072
  1149.1 46.9 %copy-start.194 = (f32[589]{0:T(1024)S(1)}, f32[589]{0:T(1024)}, u32[]{:S(2)}) copy-start(f32[589]{0:T(1024)} %param.16) | copy-start | bytes 7072
  1149.1 46.9 %copy-start.195 = (f32[589]{0:T(1024)S(1)}, f32[589]{0:T(1024)}, u32[]{:S(2)}) copy-start(f32[589]{0:T(1024)} %param.17) | copy-start | bytes 7072
  1150.6 51.8 %copy-start.94 = (f32[2,5,8,256]{3,2,1,0:T(8,128)S(1)}, f32[2,5,8,256]{3,2,1,0:T(8,128)}, u32[]{:S(2)}) copy-start(f32[2,5,8,256]{3,2,1,0:T(8,128)} %param.13) | copy-start | bytes 245764
  1189.5 12.9 %all-to-all-start.1 = ((f32[2,64,256]{2,0,1:T(2,128)}), f32[2,64,256]{2,0,1:T(2,128)S(1)}, u32[]{:S(2)}, u32[]{:S(2)}) async-start(f32[2,64,256]{2,0,1:T(2,128)} %copy.325), calls=%async_computation.2 | async-start | bytes 262144 | tf_op jit(solution)/shard_map/all_to_all | solution.py:276
  (170 other events, 471.4 us)
Sparse Core Ops, SparseCore 0:
  14.1 123.5 all-reduce.99
  140.6 58.7 all-gather.3
  227.3 32.1 all-reduce.81
  311.0 33.6 all-reduce.83
  435.0 33.4 all-reduce.85
  569.9 33.5 all-reduce.87
  644.2 120.9 all-reduce.101
  767.5 141.6 reduce-scatter.1
  1002.6 30.5 all-reduce.89
  1037.8 33.5 all-reduce.91
  1075.9 33.4 all-reduce.93
  1114.0 33.4 all-reduce.95
  1152.2 33.5 all-reduce.97
